TPU v7x, 32 devices: a whole 2x2x4 slice. The times are simulated.
32 devices in a mesh: seq: 8 (over y, x, core), head: 4 (over z).
Axes of the slice: x: 2, y: 2, z: 4, core: 2. Of those that a mesh axis runs over, the one named last changes fastest.
Arguments:
- latent: bfloat16 [8, 1024, 2048], P('seq', None, 'head'), may hold values from -6 to 6
- modulation: float32 [9, 2048], replicated, may hold values from -3 to 3
- spatial_qkv: bfloat16 [3, 2048, 2048], P(None, None, 'head')
- spatial_out: bfloat16 [2048, 2048], P('head'), may hold values from -0.125 to 0.125
- temporal_qkv: bfloat16 [3, 2048, 2048], P(None, None, 'head')
- temporal_out: bfloat16 [2048, 2048], P('head'), may hold values from -0.125 to 0.125
- hidden_weight: bfloat16 [2048, 8192], P(None, 'head'), may hold values from -0.125 to 0.125
- output_weight: bfloat16 [8192, 2048], P('head'), may hold values from -0.0625 to 0.0625
Outputs:
- block_out: bfloat16 [8, 1024, 2048], P(None, 'seq', 'head')
All inputs are finite; a program needn't handle non-finite values.
Results may differ from a plain program's by a relative error of at most 0.009.
Values may be sent and summed in bfloat16 or wider, within the bound.
No kernel may reach another device: no remote copies, remote signals or barrier semaphores. Data moves between devices by JAX's collectives and lax.ppermute only.
A program may use at most 128 MiB of HBM per device.

v0:
```python
import jax
import jax.numpy as jnp
from jax import lax
from jax.sharding import PartitionSpec as P

HD = 64


def layer_norm(values):
    average = jnp.mean(values, axis=-1, keepdims=True)
    centred = values - average
    variance = jnp.mean(centred * centred, axis=-1, keepdims=True)
    return centred * lax.rsqrt(variance + 1e-06)


def modulate(stream, modulation, offset):
    normed = layer_norm(stream.astype(jnp.float32))
    return (normed * (1.0 + modulation[offset + 1]) + modulation[offset]).astype(jnp.bfloat16)


def attend(query, keys, values):
    scores = jnp.einsum(
        "glhd,gmhd->ghlm", query, keys, preferred_element_type=jnp.float32
    ) * HD ** (-0.5)
    attn_weights = jax.nn.softmax(scores, axis=-1).astype(jnp.bfloat16)
    return jnp.einsum(
        "ghlm,gmhd->glhd", attn_weights, values, preferred_element_type=jnp.float32
    ).astype(jnp.bfloat16)


def project_three(normed, weights):
    return [
        jnp.dot(normed, weights[member], preferred_element_type=jnp.float32).astype(jnp.bfloat16)
        for member in range(3)
    ]


def column_adder(columns, portion):
    return jnp.dot(portion, columns, preferred_element_type=jnp.float32)


def per_device(
    latent,
    modulation,
    spatial_qkv,
    spatial_out,
    temporal_qkv,
    temporal_out,
    hidden_weight,
    output_weight,
):
    width_local = latent.shape[2]
    heads_local = width_local // HD
    anchor = lax.axis_index("head") * width_local
    local_rows = lax.dynamic_slice_in_dim(modulation, anchor, width_local, 1)
    full_spatial = lax.all_gather(latent, "head", axis=2, tiled=True)
    normed = modulate(full_spatial, modulation, 0)
    frames_local = latent.shape[0]
    patches = latent.shape[1]
    query, keys, values = [
        member.reshape(frames_local, patches, heads_local, HD)
        for member in project_three(normed, spatial_qkv)
    ]
    spatial = lax.map(
        lambda triple: attend(triple[0][None], triple[1][None], triple[2][None])[0],
        (query, keys, values),
    )
    spatial = spatial.reshape(frames_local, patches, width_local)
    columns = lax.all_to_all(spatial_out, "head", split_axis=1, concat_axis=0, tiled=True)
    reduced = column_adder(columns, lax.all_gather(spatial, "head", axis=2, tiled=True))
    stream_one = (latent.astype(jnp.float32) + local_rows[2] * reduced).astype(jnp.bfloat16)
    full_stream = lax.all_gather(stream_one, "head", axis=2, tiled=True)
    normed = modulate(full_stream, modulation, 3)
    stacked = jnp.stack(project_three(normed, temporal_qkv), axis=2)
    moved, stream_temporal = (
        lax.all_to_all(stacked, "seq", split_axis=1, concat_axis=0, tiled=True),
        lax.all_to_all(stream_one, "seq", split_axis=1, concat_axis=0, tiled=True),
    )
    query, keys, values = (moved[:, :, 0], moved[:, :, 1], moved[:, :, 2])
    frames = stream_temporal.shape[0]
    patches_local = stream_temporal.shape[1]

    def to_groups(tensor):
        return jnp.transpose(tensor.reshape(frames, patches_local, heads_local, HD), (1, 0, 2, 3))

    temporal = attend(to_groups(query), to_groups(keys), to_groups(values))
    temporal = jnp.transpose(temporal, (1, 0, 2, 3)).reshape(frames, patches_local, width_local)
    columns = lax.all_to_all(temporal_out, "head", split_axis=1, concat_axis=0, tiled=True)
    reduced = column_adder(columns, lax.all_gather(temporal, "head", axis=2, tiled=True))
    stream_two = (stream_temporal.astype(jnp.float32) + local_rows[5] * reduced).astype(
        jnp.bfloat16
    )
    full_two = lax.all_gather(stream_two, "head", axis=2, tiled=True)
    normed = modulate(full_two, modulation, 6)
    pre_act = jnp.dot(normed, hidden_weight, preferred_element_type=jnp.float32)
    hidden = jax.nn.gelu(pre_act, approximate=True).astype(jnp.bfloat16)
    partial_sums = jnp.dot(hidden, output_weight, preferred_element_type=jnp.float32)
    reduced = lax.psum_scatter(partial_sums, "head", scatter_dimension=2, tiled=True)
    return (stream_two.astype(jnp.float32) + local_rows[8] * reduced).astype(jnp.bfloat16)


def solution(mesh):
    in_specs = (
        P("seq", None, "head"),
        P(),
        P(None, None, "head"),
        P("head", None),
        P(None, None, "head"),
        P("head", None),
        P(None, "head"),
        P("head", None),
    )
    out_specs = P(None, "seq", "head")
    return jax.shard_map(
        per_device, mesh=mesh, in_specs=in_specs, out_specs=out_specs, check_vma=False
    )
```

profile of v0, /device:TPU:0, one launch (start us, length us, event | category | flops | bytes accessed | tf_op | source)
XLA Modules:
  0.0 838.2 jit_solution(230585978647317202)
XLA Ops:
  9.0 83.4 %all-gather.6.cloned.1.call-done = bf16[1,1024,2048]{2,1,0:T(8,128)(2,1)} async-done(((bf16[1,1024,512]{2,1,0:T(8,128)(2,1)}), bf16[1,1024,2048]{2,1,0:T(8,128)(2,1)}) %all-gather.6.cloned.1.call-update) | async-done | bytes 4194320 | tf_op jit(solution)/shard_map/all_gather | solution.py:56
  92.4 3.0 convert_reduce_fusion.2
  101.4 2.4 fusion.98
  106.3 14.6 %fusion.131 = (f32[8,1024]{1,0:T(8,128)S(1)}, f32[8,1024,1024]{1,2,0:T(8,128)}) fusion(bf16[1024,8,64]{0,2,1:T(8,128)(2,1)S(1)} %bitcast.158, bf16[1024,8,64]{0,2,1:T(8,128)(2,1)S(1)} %bitcast.159), kind=kOutput, calls=%fused_computation.121 | convolution fusion | flops 1098908672 | bytes 35684352 | tf_op jit(solution)/shard_map/while/body/eval_jaxpr/sub | solution.py:25
  120.9 13.4 %fusion.113 = bf16[8,64,1024]{2,1,0:T(8,128)(2,1)} fusion(bf16[1024,8,64]{0,2,1:T(8,128)(2,1)S(1)} %bitcast.157, f32[8,1024,1024]{1,2,0:T(8,128)} %get-tuple-element.33, f32[8,1024]{1,0:T(8,128)S(1)} %get-tuple-element.32), kind=kOutput, calls=%fused_computation.100 | convolution fusion | flops 1091043328 | bytes 35684352 | tf_op jit(solution)/shard_map/while/body/eval_jaxpr/ghlm,gmhd->glhd/dot_general | solution.py:26
  134.3 2.5 copy.49
  136.8 3.8 all-to-all-start
  141.7 100.5 %all-to-all-done = bf16[512,4,512]{0,2,1:T(8,128)(2,1)S(1)} async-done(((bf16[512,4,512]{0,2,1:T(8,128)(2,1)}), bf16[512,4,512]{0,2,1:T(8,128)(2,1)S(1)}, u32[]{:S(2)}, u32[]{:S(2)}) %all-to-all-start) | async-done | bytes 2097184 | tf_op jit(solution)/shard_map/all_to_all | solution.py:69
  244.6 12.0 %all-gather.8.cloned.1.call-done = bf16[1,1024,2048]{1,2,0:T(8,128)(2,1)} async-done(((bf16[1,1024,512]{1,2,0:T(8,128)(2,1)}), bf16[1,1024,2048]{1,2,0:T(8,128)(2,1)}) %all-gather.8.cloned.1.call-update) | async-done | bytes 4194320 | tf_op jit(solution)/shard_map/all_gather | solution.py:70
  256.6 6.2 fusion.76
  262.9 79.9 %all-gather.10.cloned.1.call-done = bf16[1,1024,2048]{2,1,0:T(8,128)(2,1)} async-done(((bf16[1,1024,512]{2,1,0:T(8,128)(2,1)}), bf16[1,1024,2048]{2,1,0:T(8,128)(2,1)}) %all-gather.10.cloned.1.call-update) | async-done | bytes 4194320 | tf_op jit(solution)/shard_map/all_gather | solution.py:72
  342.8 3.0 convert_reduce_fusion.1
  357.1 2.7 copy.52
  359.8 52.9 %all_to_all.59 = bf16[1,1024,3,512]{3,2,0,1:T(4,128)(2,1)S(1)} all-to-all(bf16[1,1024,3,512]{3,2,0,1:T(4,128)(2,1)S(1)} %copy.52), channel_id=1, replica_groups=mesh['seq'=8,'head'=4] {'seq'}, dimensions={1} | all-to-all | bytes 6291456 | tf_op jit(solution)/shard_map/all_to_all | solution.py:76
  415.7 3.0 copy.59
  420.3 3.8 copy.57
  424.1 2.8 fusion.66
  426.9 4.6 fusion.132
  432.2 3.0 copy.55
  435.2 4.2 convert_bitcast_fusion
  439.4 3.3 copy.61
  446.4 7.0 reduce.8
  455.1 3.6 all-to-all-start.1
  460.2 13.7 %all-to-all-done.1 = bf16[8,2,32768]{2,1,0:T(2,128)(2,1)S(1)} async-done(((bf16[8,2,32768]{2,1,0:T(2,128)(2,1)}), bf16[8,2,32768]{2,1,0:T(2,128)(2,1)S(1)}, u32[]{:S(2)}, u32[]{:S(2)}) %all-to-all-start.1) | async-done | bytes 1048608 | tf_op jit(solution)/shard_map/all_to_all | solution.py:77
  473.9 4.4 all-to-all-start.3
  481.1 85.2 %all-to-all-done.3 = bf16[512,4,512]{2,0,1:T(8,128)(2,1)} async-done(((bf16[512,4,512]{2,0,1:T(8,128)(2,1)}), bf16[512,4,512]{2,0,1:T(8,128)(2,1)}, u32[]{:S(2)}, u32[]{:S(2)}) %all-to-all-start.3) | async-done | bytes 2097184 | tf_op jit(solution)/shard_map/all_to_all | solution.py:88
  566.2 6.7 add_convert_fusion.1
  573.3 79.0 %all-gather.14.cloned.1.call-done = bf16[8,128,2048]{2,1,0:T(8,128)(2,1)} async-done(((bf16[8,128,512]{2,1,0:T(8,128)(2,1)}), bf16[8,128,2048]{2,1,0:T(8,128)(2,1)}) %all-gather.14.cloned.1.call-update) | async-done | bytes 4194320 | tf_op jit(solution)/shard_map/all_gather | solution.py:93
  652.3 3.0 convert_reduce_fusion
  657.0 27.8 %fusion.33 = f32[8,128,2048]{2,1,0:T(8,128)} fusion(bf16[2048,2048]{1,0:T(8,128)(2,1)} %param.15, bf16[2048,2048]{1,0:T(8,128)(2,1)} %param.14, bf16[8,128,2048]{2,1,0:T(8,128)(2,1)} %all-gather.14.cloned.1.call-done, f32[2048]{0:T(1024)S(1)} %bitcast.150, f32[2048]{0:T(1024)S(1)} %bitcast.149, f32[8,128]{1,0:T(8,128)S(1)} %add_rsqrt_fusion, ...), kind=kOutput, calls=%fused_computation.41 | convolution fusion | flops 17211326464 | bytes 29384704 | tf_op jit(solution)/shard_map/dot_general | solution.py:97
  684.8 143.3 %reduce-scatter.2.cloned.1.call-done = f32[8,128,512]{2,1,0:T(8,128)} async-done(((f32[8,128,2048]{2,1,0:T(8,128)}), f32[8,128,512]{2,1,0:T(8,128)}) %reduce-scatter.2.cloned.1.call-update) | async-done | bytes 2097168 | tf_op jit(solution)/shard_map/reduce_scatter | solution.py:98
  828.1 2.9 add_convert_fusion
  (77 shorter events, 42.4 us)
Async XLA Ops:
  6.5 85.9 %all-gather.6.cloned.1.call-start = ((), (), s32[]{:S(2)}) async-start(), calls=%async_computation.5 | async-start | bytes 5242880 | tf_op jit(solution)/shard_map/all_gather | solution.py:56
  7.3 249.4 %all-gather.8.cloned.1.call-start = ((), (), s32[]{:S(2)}) async-start(), calls=%async_computation.6 | async-start | bytes 5242880 | tf_op jit(solution)/shard_map/all_gather | solution.py:70
  92.4 3.4 copy-start
  95.8 3.1 slice-start
  97.1 1.9 slice-start.1
  120.9 13.4 %copy-start.6 = (bf16[512,2048]{1,0:T(8,128)(2,1)S(1)}, bf16[512,2048]{1,0:T(8,128)(2,1)}, u32[]{:S(2)}) copy-start(bf16[512,2048]{1,0:T(8,128)(2,1)} %param.11) | copy-start | bytes 6291460
  136.8 119.8 %copy-start.8 = (bf16[1,1024,512]{2,1,0:T(8,128)(2,1)S(1)}, bf16[1,1024,512]{2,1,0:T(8,128)(2,1)}, u32[]{:S(2)}) copy-start(bf16[1,1024,512]{2,1,0:T(8,128)(2,1)} %param.8) | copy-start | bytes 3145732
  136.8 105.4 %all-to-all-start = ((bf16[512,4,512]{0,2,1:T(8,128)(2,1)}), bf16[512,4,512]{0,2,1:T(8,128)(2,1)S(1)}, u32[]{:S(2)}, u32[]{:S(2)}) async-start(bf16[512,4,512]{0,2,1:T(8,128)(2,1)} %bitcast.133), calls=%async_computation | async-start | bytes 4194304 | tf_op jit(solution)/shard_map/all_to_all | solution.py:69
  140.6 202.2 %all-gather.10.cloned.1.call-start = ((), (), s32[]{:S(2)}) async-start(), calls=%async_computation.7 | async-start | bytes 5242880 | tf_op jit(solution)/shard_map/all_gather | solution.py:72
  262.8 303.4 %all-gather.12.cloned.1.call-start = ((), (), s32[]{:S(2)}) async-start(), calls=%async_computation.8 | async-start | bytes 5242880 | tf_op jit(solution)/shard_map/all_gather | solution.py:89
  342.8 3.4 copy-start.1
  346.3 3.1 slice-start.2
  347.5 2.3 slice-start.3
  426.9 4.7 copy-start.5
  439.4 4.8 copy-start.3
  453.5 5.2 copy-start.7
  455.1 18.9 %all-to-all-start.1 = ((bf16[8,2,32768]{2,1,0:T(2,128)(2,1)}), bf16[8,2,32768]{2,1,0:T(2,128)(2,1)S(1)}, u32[]{:S(2)}, u32[]{:S(2)}) async-start(bf16[8,2,32768]{2,1,0:T(2,128)(2,1)} %reshape.197), calls=%async_computation.1 | async-start | bytes 2097152 | tf_op jit(solution)/shard_map/all_to_all | solution.py:77
  473.9 92.3 %all-to-all-start.3 = ((bf16[512,4,512]{2,0,1:T(8,128)(2,1)}), bf16[512,4,512]{2,0,1:T(8,128)(2,1)}, u32[]{:S(2)}, u32[]{:S(2)}) async-start(bf16[512,4,512]{2,0,1:T(8,128)(2,1)} %bitcast.129), calls=%async_computation.3 | async-start | bytes 4194304 | tf_op jit(solution)/shard_map/all_to_all | solution.py:88
  478.4 173.9 %all-gather.14.cloned.1.call-start = ((), (), s32[]{:S(2)}) async-start(), calls=%async_computation.9 | async-start | bytes 5242880 | tf_op jit(solution)/shard_map/all_gather | solution.py:93
  573.0 84.0 %copy-start.10 = (f32[1,2048]{1,0:T(1,128)S(1)}, f32[1,2048]{1,0:T(1,128)}, u32[]{:S(2)}) copy-start(f32[1,2048]{1,0:T(1,128)} %get-tuple-element.31) | copy-start | bytes 24580
  573.0 84.0 %copy-start.9 = (f32[1,2048]{1,0:T(1,128)S(1)}, f32[1,2048]{1,0:T(1,128)}, u32[]{:S(2)}) copy-start(f32[1,2048]{1,0:T(1,128)} %get-tuple-element.26) | copy-start | bytes 24580
  573.0 255.1 %reduce-scatter.2.cloned.1.call-start = ((), (), s32[]{:S(2)}) async-start(), calls=%async_computation.10 | async-start | bytes 10485760 | tf_op jit(solution)/shard_map/reduce_scatter | solution.py:98
  652.3 3.4 copy-start.2
  684.8 143.3 %copy-start.4 = (bf16[8,128,512]{2,1,0:T(8,128)(2,1)S(1)}, bf16[8,128,512]{2,1,0:T(8,128)(2,1)}, u32[]{:S(2)}) copy-start(bf16[8,128,512]{2,1,0:T(8,128)(2,1)} %add_convert_fusion.1) | copy-start | bytes 3145732
Sparse Core Ops, SparseCore 0:
  8.9 83.4 all-gather.5
  134.4 122.1 all-gather.7
  263.0 79.7 all-gather.9
  444.4 121.0 all-gather.11
  573.1 79.1 all-gather.13
  685.0 143.0 reduce-scatter.1
where the time goes:
time: 849 us; the launch traced here: 838 us
  waiting for transfers between devices  598 us (70%)
  matrix products  90 us (11%)
  blocking collectives  52.9 us (6%)
  local copies, waits for them, and re-layouts  38 us (4%)
  other arithmetic  33 us (4%)
  between operations  14.2 us (2%)
  starting transfers between devices  12.4 us (1%)
    reduce_scatter x1, waiting for transfers between devices, per_device(): lax.psum_scatter(partial_sums, 'head', scatter_dimension=2, tiled=True)  143 us
    all_to_all x1, waiting for transfers between devices, per_device(): lax.all_to_all(spatial_out, 'head', split_axis=1, concat_axis=0, tiled=True)  100 us
    all_to_all x1, waiting for transfers between devices, per_device(): lax.all_to_all(temporal_out, 'head', split_axis=1, concat_axis=0, tiled=T...  85.2 us
    all_gather x1, waiting for transfers between devices, per_device(): full_spatial = lax.all_gather(latent, 'head', axis=2, tiled=True)  83.4 us
    all_gather x1, waiting for transfers between devices, per_device(): full_stream = lax.all_gather(stream_one, 'head', axis=2, tiled=True)  79.9 us
    all_gather x1, waiting for transfers between devices, per_device(): full_two = lax.all_gather(stream_two, 'head', axis=2, tiled=True)  79 us
    all_to_all x1, blocking collectives, per_device(): lax.all_to_all(stacked, 'seq', split_axis=1, concat_axis=0, tiled=True)  52.9 us
    dot_general x1, matrix products, per_device(): jnp.dot(hidden, output_weight, preferred_element_type=jnp.float32)  27.8 us
  transfers between devices with their start and end apart: 9, of which 8 were waited for; matrix products, arithmetic and copies ran while one was open for 3% of the time, Pallas kernels for 0%

commit v1 on v0

--- a/solution.py
+++ b/solution.py
@@ -53,7 +53,8 @@
     heads_local = width_local // HD
     anchor = lax.axis_index("head") * width_local
     local_rows = lax.dynamic_slice_in_dim(modulation, anchor, width_local, 1)
-    full_spatial = lax.all_gather(latent, "head", axis=2, tiled=True)
+    blocks = lax.all_gather(latent, "head")
+    full_spatial = jnp.concatenate(blocks, axis=2)
     normed = modulate(full_spatial, modulation, 0)
     frames_local = latent.shape[0]
     patches = latent.shape[1]

time: 849 us -> 854 us (level)
  no operation moved by 1% of the time
where the time goes in v1:
time: 854 us; the launch traced here: 846 us
  waiting for transfers between devices  598 us (70%)
  matrix products  90.5 us (11%)
  blocking collectives  52.7 us (6%)
  local copies, waits for them, and re-layouts  44.9 us (5%)
  other arithmetic  33.7 us (4%)
  between operations  14 us (2%)
  starting transfers between devices  12.2 us (1%)
    reduce_scatter x1, waiting for transfers between devices, per_device(): lax.psum_scatter(partial_sums, 'head', scatter_dimension=2, tiled=True)  143 us
    all_to_all x1, waiting for transfers between devices, per_device(): lax.all_to_all(spatial_out, 'head', split_axis=1, concat_axis=0, tiled=True)  101 us
    all_to_all x1, waiting for transfers between devices, per_device(): lax.all_to_all(temporal_out, 'head', split_axis=1, concat_axis=0, tiled=T...  85.1 us
    all_gather x1, waiting for transfers between devices, per_device(): blocks = lax.all_gather(latent, 'head')  83.3 us
    all_gather x1, waiting for transfers between devices, per_device(): full_stream = lax.all_gather(stream_one, 'head', axis=2, tiled=True)  79.9 us
    all_gather x1, waiting for transfers between devices, per_device(): full_two = lax.all_gather(stream_two, 'head', axis=2, tiled=True)  79.1 us
    all_to_all x1, blocking collectives, per_device(): lax.all_to_all(stacked, 'seq', split_axis=1, concat_axis=0, tiled=True)  52.7 us
    dot_general x1, matrix products, per_device(): jnp.dot(hidden, output_weight, preferred_element_type=jnp.float32)  27.8 us
  transfers between devices with their start and end apart: 9, of which 8 were waited for; matrix products, arithmetic and copies ran while one was open for 3% of the time, Pallas kernels for 0%

profile of v1, /device:TPU:0, one launch (start us, length us, event | category | flops | bytes accessed | tf_op | source)
XLA Modules:
  0.0 846.0 jit_solution(3585602246681475795)
XLA Ops:
  9.1 83.3 %all-gather.15.cloned.1.call-done = bf16[4,1024,512]{2,1,0:T(8,128)(2,1)} async-done(((bf16[1,1024,512]{2,1,0:T(8,128)(2,1)}), bf16[4,1024,512]{2,1,0:T(8,128)(2,1)}) %all-gather.15.cloned.1.call-update) | async-done | bytes 4194320 | tf_op jit(solution)/shard_map/all_gather | solution.py:56
  92.4 6.3 copy.51
  98.7 3.0 convert_reduce_fusion.2
  113.7 15.0 %fusion.130 = (f32[8,1024]{1,0:T(8,128)S(1)}, f32[8,1024,1024]{1,2,0:T(8,128)}) fusion(bf16[1024,8,64]{0,2,1:T(8,128)(2,1)S(1)} %bitcast.179, bf16[1024,8,64]{0,2,1:T(8,128)(2,1)S(1)} %bitcast.180), kind=kOutput, calls=%fused_computation.122 | convolution fusion | flops 1098908672 | bytes 35684352 | tf_op jit(solution)/shard_map/while/body/eval_jaxpr/sub | solution.py:25
  128.7 13.4 %fusion.112 = bf16[8,64,1024]{2,1,0:T(8,128)(2,1)} fusion(bf16[1024,8,64]{0,2,1:T(8,128)(2,1)S(1)} %bitcast.178, f32[8,1024,1024]{1,2,0:T(8,128)} %get-tuple-element.35, f32[8,1024]{1,0:T(8,128)S(1)} %get-tuple-element.34), kind=kOutput, calls=%fused_computation.100 | convolution fusion | flops 1091043328 | bytes 35684352 | tf_op jit(solution)/shard_map/while/body/eval_jaxpr/ghlm,gmhd->glhd/dot_general | solution.py:26
  142.1 2.5 copy.53
  144.7 3.8 all-to-all-start
  149.4 100.7 %all-to-all-done = bf16[512,4,512]{0,2,1:T(8,128)(2,1)S(1)} async-done(((bf16[512,4,512]{0,2,1:T(8,128)(2,1)}), bf16[512,4,512]{0,2,1:T(8,128)(2,1)S(1)}, u32[]{:S(2)}, u32[]{:S(2)}) %all-to-all-start) | async-done | bytes 2097184 | tf_op jit(solution)/shard_map/all_to_all | solution.py:70
  252.5 12.0 %all-gather.7.cloned.1.call-done = bf16[1,1024,2048]{1,2,0:T(8,128)(2,1)} async-done(((bf16[1,1024,512]{1,2,0:T(8,128)(2,1)}), bf16[1,1024,2048]{1,2,0:T(8,128)(2,1)}) %all-gather.7.cloned.1.call-update) | async-done | bytes 4194320 | tf_op jit(solution)/shard_map/all_gather | solution.py:71
  264.5 6.2 fusion.75
  270.8 79.9 %all-gather.9.cloned.1.call-done = bf16[1,1024,2048]{2,1,0:T(8,128)(2,1)} async-done(((bf16[1,1024,512]{2,1,0:T(8,128)(2,1)}), bf16[1,1024,2048]{2,1,0:T(8,128)(2,1)}) %all-gather.9.cloned.1.call-update) | async-done | bytes 4194320 | tf_op jit(solution)/shard_map/all_gather | solution.py:73
  350.6 3.0 convert_reduce_fusion.1
  364.9 2.7 copy.56
  367.6 52.7 %all_to_all.59 = bf16[1,1024,3,512]{3,2,0,1:T(4,128)(2,1)S(1)} all-to-all(bf16[1,1024,3,512]{3,2,0,1:T(4,128)(2,1)S(1)} %copy.56), channel_id=1, replica_groups=mesh['seq'=8,'head'=4] {'seq'}, dimensions={1} | all-to-all | bytes 6291456 | tf_op jit(solution)/shard_map/all_to_all | solution.py:77
  423.3 3.0 copy.63
  427.9 3.8 copy.61
  431.7 2.8 fusion.65
  434.6 4.6 fusion.131
  439.9 3.0 copy.59
  442.9 4.3 convert_bitcast_fusion
  447.1 3.3 copy.65
  454.4 7.0 reduce.19
  463.0 3.6 all-to-all-start.1
  468.2 13.7 %all-to-all-done.1 = bf16[8,2,32768]{2,1,0:T(2,128)(2,1)S(1)} async-done(((bf16[8,2,32768]{2,1,0:T(2,128)(2,1)}), bf16[8,2,32768]{2,1,0:T(2,128)(2,1)S(1)}, u32[]{:S(2)}, u32[]{:S(2)}) %all-to-all-start.1) | async-done | bytes 1048608 | tf_op jit(solution)/shard_map/all_to_all | solution.py:78
  481.9 4.5 all-to-all-start.3
  489.1 85.1 %all-to-all-done.3 = bf16[512,4,512]{2,0,1:T(8,128)(2,1)} async-done(((bf16[512,4,512]{2,0,1:T(8,128)(2,1)}), bf16[512,4,512]{2,0,1:T(8,128)(2,1)}, u32[]{:S(2)}, u32[]{:S(2)}) %all-to-all-start.3) | async-done | bytes 2097184 | tf_op jit(solution)/shard_map/all_to_all | solution.py:89
  574.2 6.8 add_convert_fusion.1
  581.2 79.1 %all-gather.13.cloned.1.call-done = bf16[8,128,2048]{2,1,0:T(8,128)(2,1)} async-done(((bf16[8,128,512]{2,1,0:T(8,128)(2,1)}), bf16[8,128,2048]{2,1,0:T(8,128)(2,1)}) %all-gather.13.cloned.1.call-update) | async-done | bytes 4194320 | tf_op jit(solution)/shard_map/all_gather | solution.py:94
  660.3 3.0 convert_reduce_fusion
  665.0 27.8 %fusion.29 = f32[8,128,2048]{2,1,0:T(8,128)} fusion(bf16[2048,2048]{1,0:T(8,128)(2,1)} %param.15, bf16[2048,2048]{1,0:T(8,128)(2,1)} %param.14, bf16[8,128,2048]{2,1,0:T(8,128)(2,1)} %all-gather.13.cloned.1.call-done, f32[2048]{0:T(1024)S(1)} %bitcast.171, f32[2048]{0:T(1024)S(1)} %bitcast.170, f32[8,128]{1,0:T(8,128)S(1)} %add_rsqrt_fusion, ...), kind=kOutput, calls=%fused_computation.36 | convolution fusion | flops 17211326464 | bytes 29384704 | tf_op jit(solution)/shard_map/dot_general | solution.py:98
  692.8 143.3 %reduce-scatter.2.cloned.1.call-done = f32[8,128,512]{2,1,0:T(8,128)} async-done(((f32[8,128,2048]{2,1,0:T(8,128)}), f32[8,128,512]{2,1,0:T(8,128)}) %reduce-scatter.2.cloned.1.call-update) | async-done | bytes 2097168 | tf_op jit(solution)/shard_map/reduce_scatter | solution.py:99
  836.1 2.9 add_convert_fusion
  (81 shorter events, 45.9 us)
Async XLA Ops:
  6.5 85.9 %all-gather.15.cloned.1.call-start = ((), (), s32[]{:S(2)}) async-start(), calls=%async_computation.10 | async-start | bytes 5242880 | tf_op jit(solution)/shard_map/all_gather | solution.py:56
  7.3 257.2 %all-gather.7.cloned.1.call-start = ((), (), s32[]{:S(2)}) async-start(), calls=%async_computation.5 | async-start | bytes 5242880 | tf_op jit(solution)/shard_map/all_gather | solution.py:71
  98.7 3.4 copy-start
  103.2 2.6 slice-start
  104.2 2.2 slice-start.1
  128.7 13.4 %copy-start.6 = (bf16[512,2048]{1,0:T(8,128)(2,1)S(1)}, bf16[512,2048]{1,0:T(8,128)(2,1)}, u32[]{:S(2)}) copy-start(bf16[512,2048]{1,0:T(8,128)(2,1)} %param.11) | copy-start | bytes 6291460
  144.7 119.8 %copy-start.8 = (bf16[1,1024,512]{2,1,0:T(8,128)(2,1)S(1)}, bf16[1,1024,512]{2,1,0:T(8,128)(2,1)}, u32[]{:S(2)}) copy-start(bf16[1,1024,512]{2,1,0:T(8,128)(2,1)} %param.8) | copy-start | bytes 3145732
  144.7 105.4 %all-to-all-start = ((bf16[512,4,512]{0,2,1:T(8,128)(2,1)}), bf16[512,4,512]{0,2,1:T(8,128)(2,1)S(1)}, u32[]{:S(2)}, u32[]{:S(2)}) async-start(bf16[512,4,512]{0,2,1:T(8,128)(2,1)} %bitcast.153), calls=%async_computation | async-start | bytes 4194304 | tf_op jit(solution)/shard_map/all_to_all | solution.py:70
  148.4 202.2 %all-gather.9.cloned.1.call-start = ((), (), s32[]{:S(2)}) async-start(), calls=%async_computation.6 | async-start | bytes 5242880 | tf_op jit(solution)/shard_map/all_gather | solution.py:73
  270.7 303.5 %all-gather.11.cloned.1.call-start = ((), (), s32[]{:S(2)}) async-start(), calls=%async_computation.7 | async-start | bytes 5242880 | tf_op jit(solution)/shard_map/all_gather | solution.py:90
  350.6 3.4 copy-start.1
  354.1 3.3 slice-start.2
  355.3 2.3 slice-start.3
  434.5 4.7 copy-start.5
  447.1 5.1 copy-start.3
  461.4 5.2 copy-start.7
  463.0 18.9 %all-to-all-start.1 = ((bf16[8,2,32768]{2,1,0:T(2,128)(2,1)}), bf16[8,2,32768]{2,1,0:T(2,128)(2,1)S(1)}, u32[]{:S(2)}, u32[]{:S(2)}) async-start(bf16[8,2,32768]{2,1,0:T(2,128)(2,1)} %reshape.389), calls=%async_computation.1 | async-start | bytes 2097152 | tf_op jit(solution)/shard_map/all_to_all | solution.py:78
  481.9 92.3 %all-to-all-start.3 = ((bf16[512,4,512]{2,0,1:T(8,128)(2,1)}), bf16[512,4,512]{2,0,1:T(8,128)(2,1)}, u32[]{:S(2)}, u32[]{:S(2)}) async-start(bf16[512,4,512]{2,0,1:T(8,128)(2,1)} %bitcast.147), calls=%async_computation.3 | async-start | bytes 4194304 | tf_op jit(solution)/shard_map/all_to_all | solution.py:89
  486.4 173.9 %all-gather.13.cloned.1.call-start = ((), (), s32[]{:S(2)}) async-start(), calls=%async_computation.8 | async-start | bytes 5242880 | tf_op jit(solution)/shard_map/all_gather | solution.py:94
  581.0 84.0 %copy-start.10 = (f32[1,2048]{1,0:T(1,128)S(1)}, f32[1,2048]{1,0:T(1,128)}, u32[]{:S(2)}) copy-start(f32[1,2048]{1,0:T(1,128)} %get-tuple-element.33) | copy-start | bytes 24580
  581.0 84.0 %copy-start.9 = (f32[1,2048]{1,0:T(1,128)S(1)}, f32[1,2048]{1,0:T(1,128)}, u32[]{:S(2)}) copy-start(f32[1,2048]{1,0:T(1,128)} %get-tuple-element.28) | copy-start | bytes 24580
  581.0 255.1 %reduce-scatter.2.cloned.1.call-start = ((), (), s32[]{:S(2)}) async-start(), calls=%async_computation.9 | async-start | bytes 10485760 | tf_op jit(solution)/shard_map/reduce_scatter | solution.py:99
  660.3 3.4 copy-start.2
  692.8 143.3 %copy-start.4 = (bf16[8,128,512]{2,1,0:T(8,128)(2,1)S(1)}, bf16[8,128,512]{2,1,0:T(8,128)(2,1)}, u32[]{:S(2)}) copy-start(bf16[8,128,512]{2,1,0:T(8,128)(2,1)} %add_convert_fusion.1) | copy-start | bytes 3145732
Sparse Core Ops, SparseCore 0:
  8.9 83.4 all-gather.14
  142.3 122.1 all-gather.6
  270.8 79.7 all-gather.8
  452.4 121.0 all-gather.10
  581.1 79.1 all-gather.12
  692.9 143.0 reduce-scatter.1
